TPU v7x, 32 devices: a whole 2x2x4 slice. The times are simulated.
32 devices in a mesh: blk: 8 (over z, core), grp: 4 (over y, x).
Axes of the slice: x: 2, y: 2, z: 4, core: 2. Of those that a mesh axis runs over, the one named last changes fastest.
Arguments:
- images: bfloat16 [4, 2048, 1152], P('grp', 'blk'), may hold values from -1 to 1
- texts: bfloat16 [4, 2048, 1152], P('grp', 'blk'), may hold values from -1 to 1
- labels: int32 [4, 8, 256], P('grp', 'blk'), may hold values from 0 to 255, each once within a row
- partners: int32 [2, 8], replicated, may hold values from 0 to 7, as said below
- logit_scale: float32 [], replicated, may hold values from 1 to 3
- logit_bias: float32 [], replicated, may hold values from -3 to -1
Outputs:
- image_grad: float32 [4, 2048, 1152], P('grp', 'blk')
- text_grad: float32 [4, 2048, 1152], P('grp', 'blk')
- loss: float32 [], replicated
Inputs may be any that keep to these rules, and one draw needn't show every extreme that they name: Each block's labels are a permutation of its 256 text rows. partners[r, i] is block i's partner in round r: partners[r, partners[r, i]] == i and partners[r, i] != i; no two rounds pair the same two blocks.
All inputs are finite; a program needn't handle non-finite values.
Results may differ from a plain program's by a relative error of at most 0.00035.
The roundings to bfloat16 on the way count: a program that leaves them out, or rounds other values in their place, can miss the bound.
Values may be sent and summed in bfloat16 or wider, within the bound.
A program may use at most 64 MiB of HBM per device.

v0:
```python
import functools
import jax
import jax.numpy as jnp
from jax import lax
from jax.experimental import pallas as pl
from jax.experimental.pallas import tpu as pltpu
from jax.sharding import PartitionSpec as P

MESH = pl.DeviceIdType.MESH
CHUNK_ROWS = 32
VMEM_BUDGET = 48 * 1024 * 1024
VMEM_LIMIT = 60 * 1024 * 1024


def block_weights(image_rows, text_rows, positive, logit_scale, logit_bias):
    logits = (
        logit_scale * jnp.dot(image_rows, text_rows.T, preferred_element_type=jnp.float32)
        + logit_bias
    )
    signed = jnp.where(positive, jnp.float32(1.0), jnp.float32(-1.0))
    loss_sum = jnp.sum(jax.nn.softplus(-signed * logits))
    weight = (-signed * jax.nn.sigmoid(-signed * logits)).astype(jnp.bfloat16)
    return (loss_sum, weight)


def regroup(received, partner_row):
    row_count, width = received.shape
    devices = partner_row.shape[0]
    pieces = received.reshape(row_count, devices, width // devices)
    pieces = jnp.take(pieces, partner_row, axis=1)
    return pieces.reshape(row_count, width)


def spread_body(images, texts, labels, partners, logit_scale, logit_bias):
    own_images = images[0]
    own_texts = texts[0]
    row_count = own_images.shape[0]
    columns = jnp.arange(row_count, dtype=jnp.int32)
    positive = labels[0, 0][:, None] == columns[None, :]
    nothing = jnp.zeros((row_count, row_count), dtype=bool)
    loss_sum, weight = block_weights(own_images, own_texts, positive, logit_scale, logit_bias)
    image_grad = logit_scale * jnp.dot(weight, own_texts, preferred_element_type=jnp.float32)
    text_grad = logit_scale * jnp.dot(weight.T, own_images, preferred_element_type=jnp.float32)
    for round_index in range(partners.shape[0]):
        partner_row = partners[round_index]
        spread_images, spread_texts = (
            lax.all_to_all(own_images, "blk", split_axis=1, concat_axis=1, tiled=True),
            lax.all_to_all(own_texts, "blk", split_axis=1, concat_axis=1, tiled=True),
        )
        their_images, their_texts = (
            lax.all_to_all(
                regroup(spread_images, partner_row), "blk", split_axis=1, concat_axis=1, tiled=True
            ),
            lax.all_to_all(
                regroup(spread_texts, partner_row), "blk", split_axis=1, concat_axis=1, tiled=True
            ),
        )
        round_loss, weight = block_weights(
            own_images, their_texts, nothing, logit_scale, logit_bias
        )
        image_grad = image_grad + logit_scale * jnp.dot(
            weight, their_texts, preferred_element_type=jnp.float32
        )
        _, mirror = block_weights(
            their_images, own_texts, nothing, logit_scale, logit_bias
        )
        text_grad = text_grad + logit_scale * jnp.dot(
            mirror.T, their_images, preferred_element_type=jnp.float32
        )
        loss_sum = loss_sum + round_loss
    loss_all = lax.psum(loss_sum, ("blk", "grp"))
    image_count = lax.axis_size("blk") * lax.axis_size("grp") * row_count
    loss = loss_all / jnp.float32(image_count)
    return (image_grad[None], text_grad[None], loss)


def logistic_terms(value):
    small = jnp.exp(-jnp.abs(value))
    inverse = 1.0 / (1.0 + small)
    weight = jnp.where(value >= 0, inverse, small * inverse)
    return weight, jnp.maximum(value, 0.0) + jnp.log1p(small)


def rows_dot(rows, own):
    return lax.dot_general(rows, own, (((1,), (1,)), ((), ())), preferred_element_type=jnp.float32)


def weight_dot(weight, rows):
    return lax.dot_general(
        weight, rows, (((0,), (0,)), ((), ())), preferred_element_type=jnp.float32
    )


def fold(terms):
    rows, columns = terms.shape
    total = jnp.sum(terms.reshape(rows // 8, 8, columns), axis=0)
    return sum(total[:, c : c + 128] for c in range(0, columns, 128))


def exchange_kernel(
    n, groups, rounds, edges,
    partners_ref, scale_ref, bias_ref, labels_ref, images_ref, texts_ref,
    image_acc, text_acc, loss_ref,
    own, end_images, loss_sum, group_loss, block_loss,
    own_sem, load_sem, recv_sem, send_sem, slot_sem,
    group_send, group_recv, block_send, block_recv, *buffers,
):
    chunks = len(edges) - 1
    held, slots = buffers[:chunks], buffers[chunks:]
    chips = n // 2
    me = lax.axis_index("blk")
    grp = lax.axis_index("grp")
    chip = lax.div(me, 2)
    core = lax.rem(me, 2)
    sibling = me + 1 - 2 * core
    inner = jnp.logical_and(chip > 0, chip < chips - 1)
    outer = jnp.logical_not(inner)
    up_all = chip < chips - 2
    down_all = chip > 1
    beside_end = jnp.logical_or(chip == 1, chip == chips - 2)
    end_device = jnp.where(chip == 1, me - 2, me + 2)
    scale = scale_ref[0]
    bias = bias_ref[0]

    loads = []
    for k in range(chunks):
        part = pl.ds(edges[k], edges[k + 1] - edges[k])
        loads.append([
            pltpu.make_async_copy(ref.at[0, part], held[k].at[me, i], load_sem.at[k, i])
            for i, ref in enumerate((images_ref, texts_ref))
        ])
        for copy in loads[-1]:
            copy.start()
    own_loads = [
        pltpu.make_async_copy(ref.at[0], own.at[i], own_sem.at[i])
        for i, ref in enumerate((images_ref, texts_ref))
    ]
    for copy in own_loads:
        copy.start()

    barrier = pltpu.get_barrier_semaphore()
    for step in range(1, n):
        pl.semaphore_signal(
            barrier, inc=1, device_id={"blk": lax.rem(me + step, n)}, device_id_type=MESH
        )
    for step in range(1, groups):
        pl.semaphore_signal(
            barrier, inc=1, device_id={"grp": lax.rem(grp + step, groups)}, device_id_type=MESH
        )
    pl.semaphore_wait(barrier, n - 1 + groups - 1)

    pending = []

    def copy_of(k, entry, way, target):
        return pltpu.make_async_remote_copy(
            src_ref=held[k].at[entry],
            dst_ref=held[k].at[entry],
            send_sem=send_sem.at[k, way, lax.div(entry, 2)],
            recv_sem=recv_sem.at[k, entry],
            device_id={"blk": target},
            device_id_type=MESH,
        )

    def send(k, entry, way, target, when):
        pending.append((when, lambda: copy_of(k, entry, way, target).wait_send()))
        pl.when(when)(lambda: copy_of(k, entry, way, target).start())

    def arrived(k, entry, when):
        pl.when(when)(lambda: copy_of(k, entry, 0, sibling).wait_recv())

    def send_own(k, when):
        send(k, me, 0, me + 2, jnp.logical_and(when, up_all))
        send(k, me, 1, me - 2, jnp.logical_and(when, down_all))
        send(k, me, 2, sibling, jnp.logical_and(when, inner))

    def relay(k, passing):
        for distance in range(1, chips - 1):
            below = jnp.logical_and(inner, chip >= distance)
            below = jnp.logical_and(below, up_all == passing)
            arrived(k, me - 2 * distance, below)
            if passing:
                send(k, me - 2 * distance, 0, me + 2, below)
            send(k, me - 2 * distance, 2, sibling, below)
            above = jnp.logical_and(inner, chip + distance < chips)
            above = jnp.logical_and(above, down_all == passing)
            arrived(k, me + 2 * distance, above)
            if passing:
                send(k, me + 2 * distance, 1, me - 2, above)
            send(k, me + 2 * distance, 2, sibling, above)

    def slot_copy(k):
        return pltpu.make_async_remote_copy(
            src_ref=slots[k],
            dst_ref=held[k].at[pl.ds(n, rounds)],
            send_sem=slot_sem.at[k],
            recv_sem=recv_sem.at[k, n],
            device_id={"blk": end_device},
            device_id_type=MESH,
        )

    def select(k):
        for at in range(chips):
            arrived(k, 2 * at + 1 - core, inner)

        @pl.when(beside_end)
        def _():
            for r in range(rounds):
                slots[k][r] = held[k][partners_ref[r, end_device]]
            slot_copy(k).start()

        pl.when(outer)(lambda: slot_copy(k).wait_recv())

    def add_loss(terms):
        loss_sum[...] += fold(terms)

    def compute(k):
        found = [
            held[k][jnp.where(inner, partners_ref[r, me], n + r)] for r in range(rounds)
        ]
        their_images = jnp.concatenate([rows[0] for rows in found], axis=0)
        their_texts = jnp.concatenate([rows[1] for rows in found], axis=0)
        weight, terms = logistic_terms(scale * rows_dot(their_texts, own[0]) + bias)
        pl.when(inner)(lambda: add_loss(terms))
        mirror, _ = logistic_terms(scale * rows_dot(their_images, own[1]) + bias)
        image_acc[0] += weight_dot(weight.astype(jnp.bfloat16), their_texts)
        text_acc[0] += weight_dot(mirror.astype(jnp.bfloat16), their_images)

    always = me >= 0
    for k in range(chunks):
        for copy in loads[k]:
            copy.wait()
        send_own(k, always if k < 2 else outer)

    def own_pair():
        logits = scale * rows_dot(own[1], own[0]) + bias
        positive = lax.broadcasted_iota(jnp.int32, logits.shape, 0) == labels_ref[0]
        signed = jnp.where(positive, -1.0, 1.0)
        weight, terms = logistic_terms(signed * logits)
        weight = (signed * weight).astype(jnp.bfloat16)
        loss_sum[...] = fold(terms)
        image_acc[0] = weight_dot(weight, own[1])
        text_acc[0] = jnp.dot(weight, own[0], preferred_element_type=jnp.float32)

    def end_rows():
        for k in range(chunks):
            end_images[edges[k] : edges[k + 1]] = held[k][end_device, 0]

    def end_loss(k):
        texts = jnp.concatenate([slots[k][r, 1] for r in range(rounds)], axis=0)
        _, terms = logistic_terms(scale * rows_dot(texts, end_images[...]) + bias)
        loss_sum[...] += fold(terms)

    def share(slot, position, count, axis, send, recv):
        def copy(step, index):
            return pltpu.make_async_remote_copy(
                src_ref=slot.at[index],
                dst_ref=slot.at[index],
                send_sem=send.at[step],
                recv_sem=recv.at[index],
                device_id={axis: lax.rem(position + step, count)},
                device_id_type=MESH,
            )

        def start():
            for step in range(1, count):
                copy(step, position).start()

        def finish():
            for step in range(1, count):
                copy(step, lax.rem(position + step, count)).wait_recv()
            for step in range(1, count):
                copy(step, position).wait_send()
            total = slot[0]
            for at in range(1, count):
                total = total + slot[at]
            return total

        return start, finish

    group_start, group_finish = share(group_loss, grp, groups, "grp", group_send, group_recv)
    block_start, block_finish = share(block_loss, me, n, "blk", block_send, block_recv)

    def send_loss():
        group_loss[grp] = loss_sum[...]
        group_start()
        block_loss[me] = group_finish()
        block_start()

    for copy in own_loads:
        copy.wait()
    half = chunks // 2
    ahead = 0
    for k in range(chunks):
        while ahead < min(2 * k + 2, chunks):
            relay(ahead, True)
            if 0 < ahead < chunks - 1:
                send_own(ahead + 1, inner)
            ahead += 1
        if k == 0:
            pl.when(outer)(own_pair)
            pl.when(outer)(send_loss)
        relay(k, False)
        select(k)
        if k == 0:
            pl.when(inner)(own_pair)
        compute(k)
        if k == half:
            pl.when(beside_end)(end_rows)
        if k >= half:
            for j in (2 * (k - half), 2 * (k - half) + 1):
                if j < chunks:
                    pl.when(beside_end)(functools.partial(end_loss, j))
    pl.when(inner)(send_loss)
    loss_ref[0, 0] = jnp.sum(block_finish()) / jnp.float32(n * groups * own.shape[1])

    for when, wait in pending:
        pl.when(when)(wait)
    for k in range(chunks):
        pl.when(beside_end)(lambda k=k: slot_copy(k).wait_send())


def chunk_edges(rows):
    half = CHUNK_ROWS // 2
    return [0] + list(range(half, rows, CHUNK_ROWS)) + [rows]


def gather_body(n, groups, images, texts, labels, partners, logit_scale, logit_bias):
    _, rows, width = images.shape
    rounds = partners.shape[0]
    edges = chunk_edges(rows)
    chunks = len(edges) - 1
    sizes = [edges[k + 1] - edges[k] for k in range(chunks)]
    vmem = pl.BlockSpec(memory_space=pltpu.VMEM)
    smem = pl.BlockSpec(memory_space=pltpu.SMEM)
    hbm = pl.BlockSpec(memory_space=pl.ANY)
    dma = pltpu.SemaphoreType.DMA
    grad = jax.ShapeDtypeStruct(images.shape, jnp.float32)
    image_grad, text_grad, loss = pl.pallas_call(
        functools.partial(exchange_kernel, n, groups, rounds, edges),
        out_shape=(grad, grad, jax.ShapeDtypeStruct((1, 1), jnp.float32)),
        in_specs=[smem, smem, smem, vmem, hbm, hbm],
        out_specs=(vmem, vmem, smem),
        scratch_shapes=[
            pltpu.VMEM((2, rows, width), images.dtype),
            pltpu.VMEM((rows, width), images.dtype),
            pltpu.VMEM((8, 128), jnp.float32),
            pltpu.VMEM((groups, 8, 128), jnp.float32),
            pltpu.VMEM((n, 8, 128), jnp.float32),
            dma((2,)),
            dma((chunks, 2)),
            dma((chunks, n + 1)),
            dma((chunks, 3, n // 2)),
            dma((chunks,)),
            dma((groups,)),
            dma((groups,)),
            dma((n,)),
            dma((n,)),
        ]
        + [pltpu.VMEM((n + rounds, 2, size, width), images.dtype) for size in sizes]
        + [pltpu.VMEM((rounds, 2, size, width), images.dtype) for size in sizes],
        compiler_params=pltpu.CompilerParams(
            collective_id=0, has_side_effects=True, vmem_limit_bytes=VMEM_LIMIT
        ),
    )(partners, logit_scale.reshape(1), logit_bias.reshape(1), labels, images, texts)
    return logit_scale * image_grad, logit_scale * text_grad, loss.reshape(())


def solution(mesh):
    in_specs = (P("grp", "blk", None), P("grp", "blk", None), P("grp", "blk", None), P(), P(), P())
    out_specs = (P("grp", "blk", None), P("grp", "blk", None), P())
    n, groups = mesh.shape["blk"], mesh.shape["grp"]

    def body(images, texts, labels, partners, logit_scale, logit_bias):
        _, rows, width = images.shape
        rounds = partners.shape[0]
        block = 2 * rows * width * images.dtype.itemsize
        needed = block * (n + 2 * rounds + 1) + 2 * rows * width * 4
        fits = needed <= VMEM_BUDGET and n % 2 == 0 and n >= 8
        if fits and rows % CHUNK_ROWS == 0 and rows % 128 == 0 and width % 128 == 0:
            return gather_body(
                n, groups, images, texts, labels, partners, logit_scale, logit_bias
            )
        return spread_body(images, texts, labels, partners, logit_scale, logit_bias)

    return jax.shard_map(body, mesh=mesh, in_specs=in_specs, out_specs=out_specs, check_vma=False)
```

profile of v0, /device:TPU:0, one launch (start us, length us, event | category | flops | bytes accessed | tf_op | source)
XLA Modules:
  0.0 82.1 jit_solution(7474794293777177714)
XLA Ops:
  1.9 75.1 %shard_map.85 = (f32[1,256,1152]{2,1,0:T(8,128)}, f32[1,256,1152]{2,1,0:T(8,128)}, f32[1,1]{1,0:T(1,128)}) custom-call(s32[2,8]{1,0:T(2,128)} %partners_ref.1, f32[1]{0:T(128)} %bitcast.3.scale_ref, f32[1]{0:T(128)} %bitcast.4.bias_ref, s32[1,1,256]{2,1,0:T(1,128)} %labels_ref.1, bf16[1,256,1152]{2,1,0:T(8,128)(2,1)} %images_ref.1, ...), custom_call_target="tpu_custom_call" | custom-call | tf_op jit(solution)/shard_map/pallas_call | solution.py:338
  77.1 3.2 %broadcast_multiply_fusion = (f32[1,256,1152]{2,1,0:T(8,128)}, f32[1,256,1152]{2,1,0:T(8,128)}) fusion(f32[1,256,1152]{2,1,0:T(8,128)} %get-tuple-element.7, f32[]{:T(128)} %copy.10, f32[1,256,1152]{2,1,0:T(8,128)} %get-tuple-element.6), kind=kLoop, calls=%fused_computation | loop fusion | flops 589824 | bytes 4718596 | tf_op jit(solution)/shard_map/mul | solution.py:365
where the time goes:
time: 82.3 us; the launch traced here: 82.1 us
  Pallas kernels  75.1 us (91%)
  between operations  3.75 us (5%)
  other arithmetic  3.18 us (4%)
    pallas_call x1, Pallas kernels, gather_body(): pl.pallas_call(functools.partial(exchange_kernel, n, groups, rounds, edge...  75.1 us
    mul x1, other arithmetic, gather_body(): return (logit_scale * image_grad, logit_scale * text_grad, loss.reshape(()))  3.18 us

commit v1 on v0

v1 whole, which is shorter than its diff:
```python
import functools
import jax
import jax.numpy as jnp
from jax import lax
from jax.experimental import pallas as pl
from jax.experimental.pallas import tpu as pltpu
from jax.sharding import PartitionSpec as P

MESH = pl.DeviceIdType.MESH
CHUNK_ROWS = 16
GROUP_CHUNKS = 2
TAIL_GROUPS = 2
LINE_CHIPS = 4
VMEM_BUDGET = 48 * 1024 * 1024
VMEM_LIMIT = 56 * 1024 * 1024


def block_weights(image_rows, text_rows, positive, logit_scale, logit_bias):
    logits = (
        logit_scale * jnp.dot(image_rows, text_rows.T, preferred_element_type=jnp.float32)
        + logit_bias
    )
    signed = jnp.where(positive, jnp.float32(1.0), jnp.float32(-1.0))
    loss_sum = jnp.sum(jax.nn.softplus(-signed * logits))
    weight = (-signed * jax.nn.sigmoid(-signed * logits)).astype(jnp.bfloat16)
    return (loss_sum, weight)


def regroup(received, partner_row):
    row_count, width = received.shape
    devices = partner_row.shape[0]
    pieces = received.reshape(row_count, devices, width // devices)
    pieces = jnp.take(pieces, partner_row, axis=1)
    return pieces.reshape(row_count, width)


def spread_body(images, texts, labels, partners, logit_scale, logit_bias):
    own_images = images[0]
    own_texts = texts[0]
    row_count = own_images.shape[0]
    columns = jnp.arange(row_count, dtype=jnp.int32)
    positive = labels[0, 0][:, None] == columns[None, :]
    nothing = jnp.zeros((row_count, row_count), dtype=bool)
    loss_sum, weight = block_weights(own_images, own_texts, positive, logit_scale, logit_bias)
    image_grad = logit_scale * jnp.dot(weight, own_texts, preferred_element_type=jnp.float32)
    text_grad = logit_scale * jnp.dot(weight.T, own_images, preferred_element_type=jnp.float32)
    for round_index in range(partners.shape[0]):
        partner_row = partners[round_index]
        spread_images, spread_texts = (
            lax.all_to_all(own_images, "blk", split_axis=1, concat_axis=1, tiled=True),
            lax.all_to_all(own_texts, "blk", split_axis=1, concat_axis=1, tiled=True),
        )
        their_images, their_texts = (
            lax.all_to_all(
                regroup(spread_images, partner_row), "blk", split_axis=1, concat_axis=1, tiled=True
            ),
            lax.all_to_all(
                regroup(spread_texts, partner_row), "blk", split_axis=1, concat_axis=1, tiled=True
            ),
        )
        round_loss, weight = block_weights(
            own_images, their_texts, nothing, logit_scale, logit_bias
        )
        image_grad = image_grad + logit_scale * jnp.dot(
            weight, their_texts, preferred_element_type=jnp.float32
        )
        _, mirror = block_weights(
            their_images, own_texts, nothing, logit_scale, logit_bias
        )
        text_grad = text_grad + logit_scale * jnp.dot(
            mirror.T, their_images, preferred_element_type=jnp.float32
        )
        loss_sum = loss_sum + round_loss
    loss_all = lax.psum(loss_sum, ("blk", "grp"))
    image_count = lax.axis_size("blk") * lax.axis_size("grp") * row_count
    loss = loss_all / jnp.float32(image_count)
    return (image_grad[None], text_grad[None], loss)


def logistic_terms(value):
    small = jnp.exp(-jnp.abs(value))
    inverse = 1.0 / (1.0 + small)
    weight = jnp.where(value >= 0, inverse, small * inverse)
    return weight, jnp.maximum(value, 0.0) + jnp.log1p(small)


def rows_dot(rows, own):
    return lax.dot_general(rows, own, (((1,), (1,)), ((), ())), preferred_element_type=jnp.float32)


def weight_dot(weight, rows):
    return lax.dot_general(
        weight, rows, (((0,), (0,)), ((), ())), preferred_element_type=jnp.float32
    )


def fold(terms):
    rows, columns = terms.shape
    total = jnp.sum(terms.reshape(rows // 8, 8, columns), axis=0)
    return sum(total[:, c : c + 128] for c in range(0, columns, 128))


def exchange_kernel(
    n, groups, rounds, chunk,
    partners_ref, scale_ref, bias_ref, labels_ref, images_ref, texts_ref,
    image_acc, text_acc, loss_ref,
    own, stage, slots, loss_sum, outer_loss, loss_in, loss_sent,
    own_sem, load_sem, recv_sem, send_sem, sibling_sem, forward_sem, forwarded_sem,
    slot_send, slot_recv, outer_send, outer_recv, loss_send, loss_recv,
    seen_outer, seen_line, seen_group, seen_all, *held,
):
    rows, width = own.shape[1:]
    chunks = rows // chunk
    chips = n // 2
    me = lax.axis_index("blk")
    grp = lax.axis_index("grp")
    chip = lax.div(me, 2)
    core = lax.rem(me, 2)
    sibling = me + 1 - 2 * core
    low = chip < chips // 2
    outer = jnp.logical_or(chip == 0, chip == chips - 1)
    inner = jnp.logical_not(outer)
    hub = chip == 0
    near = jnp.where(low, 0, chips - 1)
    far = chips - 1 - near
    beside = jnp.where(low, 1, chips - 2)
    across = chips - 1 - beside
    inner_count = n - 4
    scale = scale_ref[0]
    bias = bias_ref[0]

    def part(k):
        return pl.ds(k * chunk, chunk)

    def own_loads(k):
        return [
            pltpu.make_async_copy(ref.at[0, part(k)], own.at[i, part(k)], own_sem.at[k, i])
            for i, ref in enumerate((images_ref, texts_ref))
        ]

    def held_loads(k):
        return [
            pltpu.make_async_copy(ref.at[0, part(k)], held[k].at[me, i], load_sem.at[k, i])
            for i, ref in enumerate((images_ref, texts_ref))
        ]

    def each(copies, act):
        for copy in copies:
            act(copy)

    for k in range(chunks):
        each(own_loads(k), lambda copy: copy.start())
    for k in range(chunks):
        pl.when(jnp.logical_and(inner, core == k % 2))(
            lambda k=k: each(held_loads(k), lambda copy: copy.start())
        )

    barrier = pltpu.get_barrier_semaphore()

    def signal(semaphore, **device):
        pl.semaphore_signal(semaphore, inc=1, device_id=device, device_id_type=MESH)

    signal(barrier, blk=sibling)

    @pl.when(inner)
    def _():
        for other in (across, near, far):
            for c in range(2):
                signal(barrier, blk=2 * other + c)
        pl.semaphore_wait(barrier, 5)

    @pl.when(outer)
    def _():
        for c in range(2):
            signal(barrier, blk=2 * beside + c)

    @pl.when(hub)
    def _():
        for step in range(1, groups):
            signal(barrier, grp=lax.rem(grp + step, groups))
        pl.semaphore_wait(barrier, 5 + groups - 1)

    pl.when(jnp.logical_and(outer, jnp.logical_not(hub)))(lambda: pl.semaphore_wait(barrier, 5))

    def remote(src, dst, send, recv, **device):
        return pltpu.make_async_remote_copy(
            src_ref=src, dst_ref=dst, send_sem=send, recv_sem=recv,
            device_id=device, device_id_type=MESH,
        )

    def send_rows(k, target, send):
        return remote(own.at[:, part(k)], held[k].at[me], send, recv_sem.at[k], blk=target)

    def rows_arrived(k):
        block = held[k].at[pl.ds(0, n - 1)]
        return remote(block, block, send_sem.at[0], recv_sem.at[k], blk=sibling)

    def all_rows_sent(send):
        return remote(own, own, send, recv_sem.at[0], blk=sibling)

    def half_rows_sent(send):
        return remote(own.at[0], own.at[0], send, recv_sem.at[0], blk=sibling)

    def forward(k):
        return remote(held[k], held[k], forward_sem.at[k], forwarded_sem.at[k], blk=sibling)

    def slot_copy(k, c):
        return remote(
            stage.at[k // 2, c], slots.at[k], slot_send, slot_recv.at[k], blk=2 * near + c
        )

    def outer_loss_copy():
        return remote(
            outer_loss.at[0], outer_loss.at[1], outer_send, outer_recv, blk=2 * beside + core
        )

    def loss_copy(index, blk, group):
        slot = loss_in.at[index]
        return remote(slot, slot, loss_send, loss_recv, blk=blk, grp=group)

    def losses_arrived(count):
        slot = loss_in.at[pl.ds(0, count)]
        return remote(slot, slot, loss_send, loss_recv, blk=sibling)

    def losses_sent():
        return remote(loss_sent, loss_sent, loss_send, loss_recv, blk=sibling)

    def own_pair():
        logits = scale * rows_dot(own[1], own[0]) + bias
        positive = lax.broadcasted_iota(jnp.int32, logits.shape, 0) == labels_ref[0]
        signed = jnp.where(positive, -1.0, 1.0)
        weight, terms = logistic_terms(signed * logits)
        weight = (signed * weight).astype(jnp.bfloat16)
        loss_sum[...] = fold(terms)
        image_acc[0] = weight_dot(weight, own[1])
        text_acc[0] = jnp.dot(weight, own[0], preferred_element_type=jnp.float32)

    def add_pairs(their_images, their_texts, with_loss):
        weight, terms = logistic_terms(scale * rows_dot(their_texts, own[0]) + bias)
        if with_loss:
            loss_sum[...] += fold(terms)
        mirror, _ = logistic_terms(scale * rows_dot(their_images, own[1]) + bias)
        image_acc[0] += weight_dot(weight.astype(jnp.bfloat16), their_texts)
        text_acc[0] += weight_dot(mirror.astype(jnp.bfloat16), their_images)

    def joined(pieces):
        return jnp.concatenate(pieces, axis=0)

    group_list = [
        list(range(k, k + GROUP_CHUNKS)) for k in range(0, chunks, GROUP_CHUNKS)
    ]
    tail = [k for members in group_list[-TAIL_GROUPS:] for k in members]

    @pl.when(outer)
    def _():
        for k in range(chunks):
            each(own_loads(k), lambda copy: copy.wait())
            send_rows(k, 2 * across + k % 2, send_sem.at[0]).start()
            send_rows(k, 2 * beside + k % 2, send_sem.at[1]).start()
        for other in (beside, across):
            signal(seen_outer, blk=2 * other + core)
        own_pair()

        def add_slots(members, with_loss):
            for k in members:
                slot_copy(k, 0).wait_recv()
            found = [
                joined([slots[k, r, i] for r in range(rounds) for k in members])
                for i in range(2)
            ]
            add_pairs(found[0], found[1], with_loss)

        for members in group_list[:-TAIL_GROUPS]:
            add_slots(members, True)
            if members[0] == 0:
                @pl.when(hub)
                def _():
                    pl.semaphore_wait(seen_line, 1)
                    for step in range(1, groups):
                        signal(seen_group, grp=lax.rem(grp + step, groups))
                    pl.semaphore_wait(seen_group, groups - 1)
                    for other in (beside, across):
                        signal(seen_all, blk=2 * other + core)

        outer_loss[0] = jnp.sum(loss_sum[...], axis=0, keepdims=True)
        outer_loss_copy().start()
        for members in group_list[-TAIL_GROUPS:-1]:
            add_slots(members, False)
        all_rows_sent(send_sem.at[0]).wait_send()
        all_rows_sent(send_sem.at[1]).wait_send()
        outer_loss_copy().wait_send()
        for k in group_list[-1]:
            add_slots([k], False)
        losses_arrived(inner_count * groups).wait_recv()

    @pl.when(inner)
    def _():
        for k in range(chunks):
            each(own_loads(k), lambda copy: copy.wait())
            send_rows(k, 2 * across + k % 2, send_sem.at[0]).start()
            pl.when(core != k % 2)(
                lambda k=k: send_rows(k, sibling, sibling_sem).start()
            )
        own_pair()

        def select(k):
            each(held_loads(k), lambda copy: copy.wait())
            rows_arrived(k).wait_recv()
            for c in range(2):
                for r in range(rounds):
                    stage[k // 2, c, r] = held[k][partners_ref[r, 2 * near + c]]
                slot_copy(k, c).start()
            forward(k).start()

        def add_held(members):
            for c in range(2):
                @pl.when(core == c)
                def _():
                    for k in members:
                        if k % 2 == c:
                            select(k)
                    for k in members:
                        if k % 2 != c:
                            forward(k).wait_recv()
            found = [
                joined([
                    held[k][partners_ref[r, me], i] for r in range(rounds) for k in members
                ])
                for i in range(2)
            ]
            add_pairs(found[0], found[1], True)

        for members in group_list:
            add_held(members)
            if members[0] == 0:
                pl.semaphore_wait(seen_outer, 2)
                pl.when(low)(lambda: signal(seen_line, blk=2 * near + core))

        end_images = [
            joined([held[k][2 * near + c, 0] for k in range(chunks)]) for c in range(2)
        ]
        for parity in range(2):
            @pl.when(core == parity)
            def _():
                mine = [k for k in tail if k % 2 == parity]
                for c in range(2):
                    texts = joined([stage[k // 2, c, r, 1] for r in range(rounds) for k in mine])
                    _, terms = logistic_terms(scale * rows_dot(texts, end_images[c]) + bias)
                    loss_sum[...] += fold(terms)

        outer_loss_copy().wait_recv()
        pl.semaphore_wait(seen_all, 1)
        index = grp * inner_count + me - 2
        loss_in[index] = jnp.sum(loss_sum[...], axis=0, keepdims=True) + outer_loss[1]
        for step in range(groups):
            for hop in range(n):
                if step + hop > 0:
                    loss_copy(
                        index, lax.rem(me + hop, n), lax.rem(grp + step, groups)
                    ).start()
        for k in range(chunks):
            pl.when(core == k % 2)(lambda k=k: forward(k).wait_send())
        all_rows_sent(send_sem.at[0]).wait_send()
        half_rows_sent(sibling_sem).wait_send()
        remote(stage, stage, slot_send, slot_recv.at[0], blk=sibling).wait_send()
        losses_sent().wait_send()
        losses_arrived(inner_count * groups - 1).wait_recv()

    total = loss_in[0]
    for at in range(1, inner_count * groups):
        total = total + loss_in[at]
    loss_ref[0, 0] = jnp.sum(total) / jnp.float32(n * groups * rows)


def line_body(n, groups, images, texts, labels, partners, logit_scale, logit_bias):
    _, rows, width = images.shape
    rounds = partners.shape[0]
    chunk = CHUNK_ROWS
    chunks = rows // chunk
    vmem = pl.BlockSpec(memory_space=pltpu.VMEM)
    smem = pl.BlockSpec(memory_space=pltpu.SMEM)
    hbm = pl.BlockSpec(memory_space=pl.ANY)
    dma = pltpu.SemaphoreType.DMA
    regular = pltpu.SemaphoreType.REGULAR
    grad = jax.ShapeDtypeStruct(images.shape, jnp.float32)
    inner_count = n - 4
    image_grad, text_grad, loss = pl.pallas_call(
        functools.partial(exchange_kernel, n, groups, rounds, chunk),
        out_shape=(grad, grad, jax.ShapeDtypeStruct((1, 1), jnp.float32)),
        in_specs=[smem, smem, smem, vmem, hbm, hbm],
        out_specs=(vmem, vmem, smem),
        scratch_shapes=[
            pltpu.VMEM((2, rows, width), images.dtype),
            pltpu.VMEM((chunks // 2, 2, rounds, 2, chunk, width), images.dtype),
            pltpu.VMEM((chunks, rounds, 2, chunk, width), images.dtype),
            pltpu.VMEM((8, 128), jnp.float32),
            pltpu.VMEM((2, 1, 128), jnp.float32),
            pltpu.VMEM((inner_count * groups, 1, 128), jnp.float32),
            pltpu.VMEM((n * groups - 1, 1, 128), jnp.float32),
            dma((chunks, 2)),
            dma((chunks, 2)),
            dma((chunks,)),
            dma((2,)),
            dma,
            dma((chunks,)),
            dma((chunks,)),
            dma,
            dma((chunks,)),
            dma,
            dma,
            dma,
            dma,
            regular,
            regular,
            regular,
            regular,
        ]
        + [pltpu.VMEM((n, 2, chunk, width), images.dtype) for _ in range(chunks)],
        compiler_params=pltpu.CompilerParams(
            collective_id=0, has_side_effects=True, vmem_limit_bytes=VMEM_LIMIT
        ),
    )(partners, logit_scale.reshape(1), logit_bias.reshape(1), labels, images, texts)
    return logit_scale * image_grad, logit_scale * text_grad, loss.reshape(())


def solution(mesh):
    in_specs = (P("grp", "blk", None), P("grp", "blk", None), P("grp", "blk", None), P(), P(), P())
    out_specs = (P("grp", "blk", None), P("grp", "blk", None), P())
    n, groups = mesh.shape["blk"], mesh.shape["grp"]

    def body(images, texts, labels, partners, logit_scale, logit_bias):
        _, rows, width = images.shape
        rounds = partners.shape[0]
        block = 2 * rows * width * images.dtype.itemsize
        needed = block * (n + 3 * rounds + 1) + 2 * rows * width * 4
        fits = needed <= VMEM_BUDGET and n == 2 * LINE_CHIPS and groups > 1
        if fits and rows % 128 == 0 and width % 128 == 0:
            return line_body(
                n, groups, images, texts, labels, partners, logit_scale, logit_bias
            )
        return spread_body(images, texts, labels, partners, logit_scale, logit_bias)

    return jax.shard_map(body, mesh=mesh, in_specs=in_specs, out_specs=out_specs, check_vma=False)
```

time: 82.3 us -> 76 us (0.923)
  Pallas kernels: 75.1 us -> 68.8 us
    pallas_call x1, Pallas kernels: 75.1 us -> 68.8 us  [line_body(): pl.pallas_call(functools.partial(exchange_kernel, n, groups, rounds, chun...]
where the time goes in v1:
time: 76 us; the launch traced here: 75.7 us
  Pallas kernels  68.8 us (91%)
  between operations  3.75 us (5%)
  other arithmetic  3.18 us (4%)
    pallas_call x1, Pallas kernels, line_body(): pl.pallas_call(functools.partial(exchange_kernel, n, groups, rounds, chun...  68.8 us
    mul x1, other arithmetic, line_body(): return (logit_scale * image_grad, logit_scale * text_grad, loss.reshape(()))  3.18 us

profile of v1, /device:TPU:0, one launch (start us, length us, event | category | flops | bytes accessed | tf_op | source)
XLA Modules:
  0.0 75.7 jit_solution(16782687409551291827)
XLA Ops:
  1.9 68.8 %shard_map.85 = (f32[1,256,1152]{2,1,0:T(8,128)}, f32[1,256,1152]{2,1,0:T(8,128)}, f32[1,1]{1,0:T(1,128)}) custom-call(s32[2,8]{1,0:T(2,128)} %partners_ref.1, f32[1]{0:T(128)} %bitcast.3.scale_ref, f32[1]{0:T(128)} %bitcast.4.bias_ref, s32[1,1,256]{2,1,0:T(1,128)} %labels_ref.1, bf16[1,256,1152]{2,1,0:T(8,128)(2,1)} %images_ref.1, ...), custom_call_target="tpu_custom_call" | custom-call | tf_op jit(solution)/shard_map/pallas_call | solution.py:387
  70.7 3.2 %broadcast_multiply_fusion = (f32[1,256,1152]{2,1,0:T(8,128)}, f32[1,256,1152]{2,1,0:T(8,128)}) fusion(f32[1,256,1152]{2,1,0:T(8,128)} %get-tuple-element.7, f32[]{:T(128)} %copy.10, f32[1,256,1152]{2,1,0:T(8,128)} %get-tuple-element.6), kind=kLoop, calls=%fused_computation | loop fusion | flops 589824 | bytes 4718596 | tf_op jit(solution)/shard_map/mul | solution.py:423

commit v2 on v1

--- a/solution.py
+++ b/solution.py
@@ -12,7 +12,8 @@
 TAIL_GROUPS = 2
 LINE_CHIPS = 4
 VMEM_BUDGET = 48 * 1024 * 1024
-VMEM_LIMIT = 56 * 1024 * 1024
+VMEM_LIMIT = 32 * 1024 * 1024
+FINISH_LIMIT = 16 * 1024 * 1024
 
 
 def block_weights(image_rows, text_rows, positive, logit_scale, logit_bias):
@@ -102,9 +103,9 @@
 
 def exchange_kernel(
     n, groups, rounds, chunk,
-    partners_ref, scale_ref, bias_ref, labels_ref, images_ref, texts_ref,
+    partners_in, scale_ref, bias_ref, labels_in, images_ref, texts_ref,
     image_acc, text_acc, loss_ref,
-    own, stage, slots, loss_sum, outer_loss, loss_in, loss_sent,
+    partners_ref, labels_ref, small_sem, own, stage, slots, loss_sum, outer_loss, loss_in, loss_sent,
     own_sem, load_sem, recv_sem, send_sem, sibling_sem, forward_sem, forwarded_sem,
     slot_send, slot_recv, outer_send, outer_recv, loss_send, loss_recv,
     seen_outer, seen_line, seen_group, seen_all, *held,
@@ -126,9 +127,6 @@
     beside = jnp.where(low, 1, chips - 2)
     across = chips - 1 - beside
     inner_count = n - 4
-    scale = scale_ref[0]
-    bias = bias_ref[0]
-
     def part(k):
         return pl.ds(k * chunk, chunk)
 
@@ -148,8 +146,15 @@
         for copy in copies:
             act(copy)
 
+    small = [
+        pltpu.make_async_copy(src, dst, small_sem.at[i])
+        for i, (src, dst) in enumerate((
+            (labels_in.at[0], labels_ref), (partners_in, partners_ref),
+        ))
+    ]
     for k in range(chunks):
         each(own_loads(k), lambda copy: copy.start())
+    each(small, lambda copy: copy.start())
     for k in range(chunks):
         pl.when(jnp.logical_and(inner, core == k % 2))(
             lambda k=k: each(held_loads(k), lambda copy: copy.start())
@@ -226,8 +231,9 @@
         return remote(loss_sent, loss_sent, loss_send, loss_recv, blk=sibling)
 
     def own_pair():
+        scale, bias = scale_ref[...], bias_ref[...]
         logits = scale * rows_dot(own[1], own[0]) + bias
-        positive = lax.broadcasted_iota(jnp.int32, logits.shape, 0) == labels_ref[0]
+        positive = lax.broadcasted_iota(jnp.int32, logits.shape, 0) == labels_ref[...]
         signed = jnp.where(positive, -1.0, 1.0)
         weight, terms = logistic_terms(signed * logits)
         weight = (signed * weight).astype(jnp.bfloat16)
@@ -235,13 +241,16 @@
         image_acc[0] = weight_dot(weight, own[1])
         text_acc[0] = jnp.dot(weight, own[0], preferred_element_type=jnp.float32)
 
-    def add_pairs(their_images, their_texts, with_loss):
+    def add_pairs(their_images, their_texts, with_loss, last):
+        scale, bias = scale_ref[...], bias_ref[...]
         weight, terms = logistic_terms(scale * rows_dot(their_texts, own[0]) + bias)
         if with_loss:
             loss_sum[...] += fold(terms)
         mirror, _ = logistic_terms(scale * rows_dot(their_images, own[1]) + bias)
-        image_acc[0] += weight_dot(weight.astype(jnp.bfloat16), their_texts)
-        text_acc[0] += weight_dot(mirror.astype(jnp.bfloat16), their_images)
+        image_sum = image_acc[0] + weight_dot(weight.astype(jnp.bfloat16), their_texts)
+        text_sum = text_acc[0] + weight_dot(mirror.astype(jnp.bfloat16), their_images)
+        image_acc[0] = scale * image_sum if last else image_sum
+        text_acc[0] = scale * text_sum if last else text_sum
 
     def joined(pieces):
         return jnp.concatenate(pieces, axis=0)
@@ -259,16 +268,17 @@
             send_rows(k, 2 * beside + k % 2, send_sem.at[1]).start()
         for other in (beside, across):
             signal(seen_outer, blk=2 * other + core)
+        each(small, lambda copy: copy.wait())
         own_pair()
 
-        def add_slots(members, with_loss):
+        def add_slots(members, with_loss, last=False):
             for k in members:
                 slot_copy(k, 0).wait_recv()
             found = [
                 joined([slots[k, r, i] for r in range(rounds) for k in members])
                 for i in range(2)
             ]
-            add_pairs(found[0], found[1], with_loss)
+            add_pairs(found[0], found[1], with_loss, last)
 
         for members in group_list[:-TAIL_GROUPS]:
             add_slots(members, True)
@@ -290,7 +300,7 @@
         all_rows_sent(send_sem.at[1]).wait_send()
         outer_loss_copy().wait_send()
         for k in group_list[-1]:
-            add_slots([k], False)
+            add_slots([k], False, k == chunks - 1)
         losses_arrived(inner_count * groups).wait_recv()
 
     @pl.when(inner)
@@ -301,6 +311,7 @@
             pl.when(core != k % 2)(
                 lambda k=k: send_rows(k, sibling, sibling_sem).start()
             )
+        each(small, lambda copy: copy.wait())
         own_pair()
 
         def select(k):
@@ -328,7 +339,7 @@
                 ])
                 for i in range(2)
             ]
-            add_pairs(found[0], found[1], True)
+            add_pairs(found[0], found[1], True, members[-1] == chunks - 1)
 
         for members in group_list:
             add_held(members)
@@ -345,7 +356,8 @@
                 mine = [k for k in tail if k % 2 == parity]
                 for c in range(2):
                     texts = joined([stage[k // 2, c, r, 1] for r in range(rounds) for k in mine])
-                    _, terms = logistic_terms(scale * rows_dot(texts, end_images[c]) + bias)
+                    logits = scale_ref[...] * rows_dot(texts, end_images[c]) + bias_ref[...]
+                    _, terms = logistic_terms(logits)
                     loss_sum[...] += fold(terms)
 
         outer_loss_copy().wait_recv()
@@ -369,7 +381,27 @@
     total = loss_in[0]
     for at in range(1, inner_count * groups):
         total = total + loss_in[at]
-    loss_ref[0, 0] = jnp.sum(total) / jnp.float32(n * groups * rows)
+    loss_ref[...] = total
+
+
+def finish_kernel(
+    image_count, image_in, text_in, loss_in, image_out, text_out, loss_out, loss_cell, sems
+):
+    copies = [
+        pltpu.make_async_copy(image_in, image_out, sems.at[0]),
+        pltpu.make_async_copy(text_in, text_out, sems.at[1]),
+        pltpu.make_async_copy(loss_cell, loss_out, sems.at[2]),
+    ]
+    copies[0].start()
+    copies[1].start()
+    loss_cell[0, 0] = jnp.sum(loss_in[...]) / jnp.float32(image_count)
+    copies[2].start()
+    for copy in copies:
+        copy.wait()
+
+
+def keep(array):
+    return pltpu.with_memory_space_constraint(array, pltpu.HBM)
 
 
 def line_body(n, groups, images, texts, labels, partners, logit_scale, logit_bias):
@@ -384,12 +416,15 @@
     regular = pltpu.SemaphoreType.REGULAR
     grad = jax.ShapeDtypeStruct(images.shape, jnp.float32)
     inner_count = n - 4
-    image_grad, text_grad, loss = pl.pallas_call(
+    image_sum, text_sum, loss_sum = pl.pallas_call(
         functools.partial(exchange_kernel, n, groups, rounds, chunk),
-        out_shape=(grad, grad, jax.ShapeDtypeStruct((1, 1), jnp.float32)),
-        in_specs=[smem, smem, smem, vmem, hbm, hbm],
-        out_specs=(vmem, vmem, smem),
+        out_shape=(grad, grad, jax.ShapeDtypeStruct((1, 128), jnp.float32)),
+        in_specs=[hbm, smem, smem, hbm, hbm, hbm],
+        out_specs=(vmem, vmem, vmem),
         scratch_shapes=[
+            pltpu.SMEM((rounds, n), jnp.int32),
+            pltpu.VMEM((1, rows), jnp.int32),
+            dma((4,)),
             pltpu.VMEM((2, rows, width), images.dtype),
             pltpu.VMEM((chunks // 2, 2, rounds, 2, chunk, width), images.dtype),
             pltpu.VMEM((chunks, rounds, 2, chunk, width), images.dtype),
@@ -419,8 +454,19 @@
         compiler_params=pltpu.CompilerParams(
             collective_id=0, has_side_effects=True, vmem_limit_bytes=VMEM_LIMIT
         ),
-    )(partners, logit_scale.reshape(1), logit_bias.reshape(1), labels, images, texts)
-    return logit_scale * image_grad, logit_scale * text_grad, loss.reshape(())
+    )(
+        keep(partners), logit_scale, logit_bias,
+        keep(labels), keep(images), keep(texts),
+    )
+    image_grad, text_grad, loss = pl.pallas_call(
+        functools.partial(finish_kernel, n * groups * rows),
+        out_shape=(grad, grad, jax.ShapeDtypeStruct((1, 1), jnp.float32)),
+        in_specs=[vmem, vmem, vmem],
+        out_specs=(hbm, hbm, hbm),
+        scratch_shapes=[pltpu.SMEM((1, 1), jnp.float32), dma((3,))],
+        compiler_params=pltpu.CompilerParams(vmem_limit_bytes=FINISH_LIMIT),
+    )(image_sum, text_sum, loss_sum)
+    return image_grad, text_grad, loss.reshape(())
 
 
 def solution(mesh):

time: 76 us -> 70.5 us (0.928)
  other arithmetic: 3.18 us -> 0 us
  between operations: 3.75 us -> 2.11 us
    mul x1 -> x0, other arithmetic: 3.18 us -> none  [line_body(): return (logit_scale * image_grad, logit_scale * text_grad, loss.reshape(()))]
    pallas_call x1, Pallas kernels: 68.8 us -> 66.7 us  [line_body(): pl.pallas_call(functools.partial(exchange_kernel, n, groups, rounds, chun...]
    pallas_call x0 -> x1, Pallas kernels: none -> 1.44 us  [line_body(): pl.pallas_call(functools.partial(finish_kernel, n * groups * rows), out_s...]
where the time goes in v2:
time: 70.5 us; the launch traced here: 70.3 us
  Pallas kernels  68.2 us (97%)
  between operations  2.11 us (3%)
    pallas_call x1, Pallas kernels, line_body(): pl.pallas_call(functools.partial(exchange_kernel, n, groups, rounds, chun...  66.7 us
    pallas_call x1, Pallas kernels, line_body(): pl.pallas_call(functools.partial(finish_kernel, n * groups * rows), out_s...  1.44 us

profile of v2, /device:TPU:0, one launch (start us, length us, event | category | flops | bytes accessed | tf_op | source)
XLA Modules:
  0.0 70.3 jit_solution(5480177878239899222)
XLA Ops:
  1.9 66.7 %shard_map.85 = (f32[1,256,1152]{2,1,0:T(8,128)S(1)}, f32[1,256,1152]{2,1,0:T(8,128)S(1)}, f32[1,128]{1,0:T(1,128)S(1)}) custom-call(s32[2,8]{1,0:T(2,128)} %partners_in.1, f32[]{:T(128)S(6)} %copy.9.scale_ref, f32[]{:T(128)S(6)} %copy.10.bias_ref, s32[1,1,256]{2,1,0:T(1,128)} %labels_in.1, bf16[1,256,1152]{2,1,0:T(8,128)(2,1)} %images_ref.1, ...), custom_call_target="tpu_custom_call" | custom-call | tf_op jit(solution)/shard_map/pallas_call | solution.py:419
  68.7 1.4 %shard_map.86 = (f32[1,256,1152]{2,1,0:T(8,128)}, f32[1,256,1152]{2,1,0:T(8,128)}, f32[1,1]{1,0:T(1,128)}) custom-call(f32[1,256,1152]{2,1,0:T(8,128)S(1)} %get-tuple-element.9.image_in, f32[1,256,1152]{2,1,0:T(8,128)S(1)} %get-tuple-element.10.text_in, f32[1,128]{1,0:T(1,128)S(1)} %get-tuple-element.11.loss_in), custom_call_target="tpu_custom_call" | custom-call | tf_op jit(solution)/shard_map/pallas_call | solution.py:461

commit v3 on v2

v3 whole, which is shorter than its diff:
```python
import functools
import jax
import jax.numpy as jnp
from jax import lax
from jax.experimental import pallas as pl
from jax.experimental.pallas import tpu as pltpu
from jax.sharding import PartitionSpec as P

MESH = pl.DeviceIdType.MESH
CHUNK_ROWS = 16
GROUP_CHUNKS = 4
AHEAD_CHUNKS = 12
LINE_CHIPS = 4
VMEM_BUDGET = 48 * 1024 * 1024
VMEM_LIMIT = 32 * 1024 * 1024
FINISH_LIMIT = 16 * 1024 * 1024
FINISH_STEPS = 2


def block_weights(image_rows, text_rows, positive, logit_scale, logit_bias):
    logits = (
        logit_scale * jnp.dot(image_rows, text_rows.T, preferred_element_type=jnp.float32)
        + logit_bias
    )
    signed = jnp.where(positive, jnp.float32(1.0), jnp.float32(-1.0))
    loss_sum = jnp.sum(jax.nn.softplus(-signed * logits))
    weight = (-signed * jax.nn.sigmoid(-signed * logits)).astype(jnp.bfloat16)
    return (loss_sum, weight)


def regroup(received, partner_row):
    row_count, width = received.shape
    devices = partner_row.shape[0]
    pieces = received.reshape(row_count, devices, width // devices)
    pieces = jnp.take(pieces, partner_row, axis=1)
    return pieces.reshape(row_count, width)


def spread_body(images, texts, labels, partners, logit_scale, logit_bias):
    own_images = images[0]
    own_texts = texts[0]
    row_count = own_images.shape[0]
    columns = jnp.arange(row_count, dtype=jnp.int32)
    positive = labels[0, 0][:, None] == columns[None, :]
    nothing = jnp.zeros((row_count, row_count), dtype=bool)
    loss_sum, weight = block_weights(own_images, own_texts, positive, logit_scale, logit_bias)
    image_grad = logit_scale * jnp.dot(weight, own_texts, preferred_element_type=jnp.float32)
    text_grad = logit_scale * jnp.dot(weight.T, own_images, preferred_element_type=jnp.float32)
    for round_index in range(partners.shape[0]):
        partner_row = partners[round_index]
        spread_images, spread_texts = (
            lax.all_to_all(own_images, "blk", split_axis=1, concat_axis=1, tiled=True),
            lax.all_to_all(own_texts, "blk", split_axis=1, concat_axis=1, tiled=True),
        )
        their_images, their_texts = (
            lax.all_to_all(
                regroup(spread_images, partner_row), "blk", split_axis=1, concat_axis=1, tiled=True
            ),
            lax.all_to_all(
                regroup(spread_texts, partner_row), "blk", split_axis=1, concat_axis=1, tiled=True
            ),
        )
        round_loss, weight = block_weights(
            own_images, their_texts, nothing, logit_scale, logit_bias
        )
        image_grad = image_grad + logit_scale * jnp.dot(
            weight, their_texts, preferred_element_type=jnp.float32
        )
        _, mirror = block_weights(
            their_images, own_texts, nothing, logit_scale, logit_bias
        )
        text_grad = text_grad + logit_scale * jnp.dot(
            mirror.T, their_images, preferred_element_type=jnp.float32
        )
        loss_sum = loss_sum + round_loss
    loss_all = lax.psum(loss_sum, ("blk", "grp"))
    image_count = lax.axis_size("blk") * lax.axis_size("grp") * row_count
    loss = loss_all / jnp.float32(image_count)
    return (image_grad[None], text_grad[None], loss)


def logistic_terms(value):
    small = jnp.exp(-jnp.abs(value))
    inverse = 1.0 / (1.0 + small)
    weight = jnp.where(value >= 0, inverse, small * inverse)
    return weight, jnp.maximum(value, 0.0) + jnp.log1p(small)


def rows_dot(rows, own):
    return lax.dot_general(rows, own, (((1,), (1,)), ((), ())), preferred_element_type=jnp.float32)


def weight_dot(weight, rows):
    return lax.dot_general(
        weight, rows, (((0,), (0,)), ((), ())), preferred_element_type=jnp.float32
    )


def fold(terms):
    rows, columns = terms.shape
    total = jnp.sum(terms.reshape(rows // 8, 8, columns), axis=0)
    return sum(total[:, c : c + 128] for c in range(0, columns, 128))


def exchange_kernel(
    n, groups, rounds, chunk,
    partners_in, scale_ref, bias_ref, labels_in, images_ref, texts_ref,
    image_acc, text_acc, tail_weight, tail_rows, loss_ref,
    partners_ref, labels_ref, small_sem, own, stage, slots, loss_sum, outer_loss, loss_in, loss_sent,
    own_sem, load_sem, recv_sem, send_sem, sibling_sem, forward_sem, forwarded_sem,
    slot_send, slot_recv, outer_send, outer_recv, loss_send, loss_recv,
    seen_outer, seen_line, seen_group, seen_all, *held,
):
    rows = own.shape[1]
    half = rows // chunk
    chunks = 2 * half
    chips = n // 2
    me = lax.axis_index("blk")
    grp = lax.axis_index("grp")
    chip = lax.div(me, 2)
    core = lax.rem(me, 2)
    sibling = me + 1 - 2 * core
    low = chip < chips // 2
    outer = jnp.logical_or(chip == 0, chip == chips - 1)
    inner = jnp.logical_not(outer)
    hub = chip == 0
    near = jnp.where(low, 0, chips - 1)
    far = chips - 1 - near
    beside = jnp.where(low, 1, chips - 2)
    across = chips - 1 - beside
    inner_count = n - 4
    sources = (images_ref, texts_ref)

    def kind(k):
        return 1 if k < half else 0

    def part(k):
        return pl.ds(k % half * chunk, chunk)

    pieces, first = [], 0
    while first < half:
        count = min(max(first, 1), half - first)
        pieces.append((first, count))
        first += count
    pieces.append((half, half))

    def own_load(p):
        first, count = pieces[p]
        piece = pl.ds(first % half * chunk, count * chunk)
        i = kind(first)
        return pltpu.make_async_copy(sources[i].at[0, piece], own.at[i, piece], own_sem.at[p])

    def own_ready(k):
        for p, (first, _) in enumerate(pieces):
            if first == k:
                own_load(p).wait()

    def held_load(k):
        return pltpu.make_async_copy(
            sources[kind(k)].at[0, part(k)], held[k].at[me], load_sem.at[k]
        )

    small = [
        pltpu.make_async_copy(labels_in.at[0], labels_ref, small_sem.at[0]),
        pltpu.make_async_copy(partners_in, partners_ref, small_sem.at[1]),
    ]
    barrier = pltpu.get_barrier_semaphore()

    def signal(semaphore, **device):
        pl.semaphore_signal(semaphore, inc=1, device_id=device, device_id_type=MESH)

    own_load(0).start()

    @pl.when(inner)
    def _():
        for other in (across, near, far):
            for c in range(2):
                signal(barrier, blk=2 * other + c)

    @pl.when(outer)
    def _():
        for c in range(2):
            signal(barrier, blk=2 * beside + c)

    signal(barrier, blk=sibling)

    @pl.when(hub)
    def _():
        for step in range(1, groups):
            signal(barrier, grp=lax.rem(grp + step, groups))

    for p in range(1, len(pieces)):
        own_load(p).start()
    for copy in small:
        copy.start()
    pl.when(hub)(lambda: pl.semaphore_wait(barrier, 5 + groups - 1))
    pl.when(jnp.logical_not(hub))(lambda: pl.semaphore_wait(barrier, 5))

    def remote(src, dst, send, recv, **device):
        return pltpu.make_async_remote_copy(
            src_ref=src, dst_ref=dst, send_sem=send, recv_sem=recv,
            device_id=device, device_id_type=MESH,
        )

    def send_rows(k, target, send):
        return remote(
            own.at[kind(k), part(k)], held[k].at[me], send, recv_sem.at[k], blk=target
        )

    def rows_arrived(k):
        block = held[k].at[pl.ds(0, n - 1)]
        return remote(block, block, send_sem.at[0], recv_sem.at[k], blk=sibling)

    def all_rows_sent(send):
        return remote(own, own, send, recv_sem.at[0], blk=sibling)

    def half_rows_sent(send):
        return remote(own.at[0], own.at[0], send, recv_sem.at[0], blk=sibling)

    def forward(k):
        return remote(held[k], held[k], forward_sem.at[k], forwarded_sem.at[k], blk=sibling)

    def slot_copy(k, c):
        return remote(
            stage.at[k // 2, c], slots.at[k], slot_send, slot_recv.at[k], blk=2 * near + c
        )

    def outer_loss_copy():
        return remote(
            outer_loss.at[0], outer_loss.at[1], outer_send, outer_recv, blk=2 * beside + core
        )

    def loss_copy(index, blk, group):
        slot = loss_in.at[index]
        return remote(slot, slot, loss_send, loss_recv, blk=blk, grp=group)

    def losses_arrived(count):
        slot = loss_in.at[pl.ds(0, count)]
        return remote(slot, slot, loss_send, loss_recv, blk=sibling)

    def losses_sent():
        return remote(loss_sent, loss_sent, loss_send, loss_recv, blk=sibling)

    def own_pair():
        logits = scale_ref[...] * rows_dot(own[1], own[0]) + bias_ref[...]
        positive = lax.broadcasted_iota(jnp.int32, logits.shape, 0) == labels_ref[...]
        signed = jnp.where(positive, -1.0, 1.0)
        weight, terms = logistic_terms(signed * logits)
        weight = (signed * weight).astype(jnp.bfloat16)
        loss_sum[...] = fold(terms)
        image_acc[0] = weight_dot(weight, own[1])
        text_acc[0] = jnp.dot(weight, own[0], preferred_element_type=jnp.float32)

    def their_weight(found, i):
        logits = scale_ref[...] * rows_dot(found, own[1 - i]) + bias_ref[...]
        weight, terms = logistic_terms(logits)
        if i == 1:
            loss_sum[...] += fold(terms)
        return weight.astype(jnp.bfloat16)

    def add_pairs(found, i):
        acc = image_acc if i == 1 else text_acc
        acc[0] += weight_dot(their_weight(found, i), found)

    def leave_pairs(found, i):
        tail_weight[...] = their_weight(found, i)
        tail_rows[...] = found

    def joined(parts):
        return jnp.concatenate(parts, axis=0)

    def loss_total():
        total = loss_in[0]
        for at in range(1, inner_count * groups):
            total = total + loss_in[at]
        loss_ref[...] = total

    def in_groups(first, last):
        return [
            list(range(k, min(k + GROUP_CHUNKS, last)))
            for k in range(first, last, GROUP_CHUNKS)
        ]

    text_groups = in_groups(0, half)
    image_groups = in_groups(half, chunks - 1)
    loss_group = image_groups[-2]

    @pl.when(outer)
    def _():
        def send_chunks(first, last):
            for k in range(first, min(last, chunks)):
                send_rows(k, 2 * across + k % 2, send_sem.at[0]).start()
                send_rows(k, 2 * beside + k % 2, send_sem.at[1]).start()

        for k in range(AHEAD_CHUNKS):
            own_ready(k)
            send_chunks(k, k + 1)
        for k in range(AHEAD_CHUNKS, chunks):
            own_ready(k)
        for other in (beside, across):
            signal(seen_outer, blk=2 * other + core)
        for copy in small:
            copy.wait()
        own_pair()

        def slot_rows(members):
            for k in members:
                slot_copy(k, 0).wait_recv()
                send_chunks(k + AHEAD_CHUNKS, k + AHEAD_CHUNKS + 1)
            return joined([slots[k, r] for r in range(rounds) for k in members])

        for members in text_groups:
            add_pairs(slot_rows(members), 1)
            if members[0] == 0:
                @pl.when(hub)
                def _():
                    pl.semaphore_wait(seen_line, 1)
                    for step in range(1, groups):
                        signal(seen_group, grp=lax.rem(grp + step, groups))
                    pl.semaphore_wait(seen_group, groups - 1)
                    for other in (beside, across):
                        signal(seen_all, blk=2 * other + core)

        outer_loss[0] = jnp.sum(loss_sum[...], axis=0, keepdims=True)
        outer_loss_copy().start()
        image_acc[0] = scale_ref[...] * image_acc[0]
        for members in image_groups:
            add_pairs(slot_rows(members), 0)
        outer_loss_copy().wait_send()
        losses_arrived(inner_count * groups).wait_recv()
        loss_total()
        all_rows_sent(send_sem.at[0]).wait_send()
        all_rows_sent(send_sem.at[1]).wait_send()
        leave_pairs(slot_rows([chunks - 1]), 0)

    @pl.when(inner)
    def _():
        for k in range(chunks):
            own_ready(k)
            send_rows(k, 2 * across + k % 2, send_sem.at[0]).start()
            pl.when(core != k % 2)(
                lambda k=k: send_rows(k, sibling, sibling_sem).start()
            )
        for k in range(chunks):
            pl.when(core == k % 2)(lambda k=k: held_load(k).start())
        for copy in small:
            copy.wait()
        own_pair()

        def select(k):
            held_load(k).wait()
            rows_arrived(k).wait_recv()
            for c in range(2):
                for r in range(rounds):
                    stage[k // 2, c, r] = held[k][partners_ref[r, 2 * near + c]]
                slot_copy(k, c).start()
            forward(k).start()

        def held_rows(members):
            for c in range(2):
                @pl.when(core == c)
                def _():
                    for k in members:
                        if k % 2 == c:
                            select(k)
                    for k in members:
                        if k % 2 != c:
                            forward(k).wait_recv()
            return joined([held[k][partners_ref[r, me]] for r in range(rounds) for k in members])

        def send_loss():
            outer_loss_copy().wait_recv()
            pl.semaphore_wait(seen_all, 1)
            index = grp * inner_count + me - 2
            loss_in[index] = jnp.sum(loss_sum[...], axis=0, keepdims=True) + outer_loss[1]
            for group in range(groups):
                for blk in (0, 1, n - 2, n - 1):
                    loss_copy(index, blk, group).start()
            for step in range(groups):
                for hop in range(inner_count):
                    if step + hop > 0:
                        blk = 2 + lax.rem(me - 2 + hop, inner_count)
                        loss_copy(index, blk, lax.rem(grp + step, groups)).start()

        for members in text_groups:
            add_pairs(held_rows(members), 1)
            if members[0] == 0:
                pl.semaphore_wait(seen_outer, 2)
                pl.when(low)(lambda: signal(seen_line, blk=2 * near + core))
        image_acc[0] = scale_ref[...] * image_acc[0]
        for members in image_groups:
            add_pairs(held_rows(members), 0)
            if members == loss_group:
                send_loss()
        losses_sent().wait_send()
        losses_arrived(inner_count * groups - 1).wait_recv()
        loss_total()
        for k in range(chunks - 2):
            pl.when(core == k % 2)(lambda k=k: forward(k).wait_send())
        leave_pairs(held_rows([chunks - 1]), 0)
        for k in range(chunks - 2, chunks):
            pl.when(core == k % 2)(lambda k=k: forward(k).wait_send())
        all_rows_sent(send_sem.at[0]).wait_send()
        half_rows_sent(sibling_sem).wait_send()
        remote(stage, stage, slot_send, slot_recv.at[0], blk=sibling).wait_send()


def finish_kernel(
    image_count, scale_ref, image_in, text_in, weight, tail, loss_in,
    image_out, text_out, loss_out, ready, loss_cell, image_sem, sems, loss_sem,
):
    rows = text_in.shape[1]
    copies = [pltpu.make_async_copy(image_in, image_out, image_sem)]
    copies[-1].start()
    for at in range(FINISH_STEPS):
        part = pl.ds(at * (rows // FINISH_STEPS), rows // FINISH_STEPS)
        total = text_in[0, part] + weight_dot(weight[:, part], tail[...])
        ready[part] = scale_ref[...] * total
        copies.append(pltpu.make_async_copy(ready.at[part], text_out.at[0, part], sems.at[at]))
        copies[-1].start()
    loss_cell[0, 0] = jnp.sum(loss_in[...]) / jnp.float32(image_count)
    copies.append(pltpu.make_async_copy(loss_cell, loss_out, loss_sem))
    copies[-1].start()
    for copy in copies:
        copy.wait()


def keep(array):
    return pltpu.with_memory_space_constraint(array, pltpu.HBM)


def line_body(n, groups, images, texts, labels, partners, logit_scale, logit_bias):
    _, rows, width = images.shape
    rounds = partners.shape[0]
    chunk = CHUNK_ROWS
    chunks = 2 * rows // chunk
    vmem = pl.BlockSpec(memory_space=pltpu.VMEM)
    smem = pl.BlockSpec(memory_space=pltpu.SMEM)
    hbm = pl.BlockSpec(memory_space=pl.ANY)
    dma = pltpu.SemaphoreType.DMA
    regular = pltpu.SemaphoreType.REGULAR
    grad = jax.ShapeDtypeStruct(images.shape, jnp.float32)
    inner_count = n - 4
    image_sum, text_sum, weight, tail, loss_sum = pl.pallas_call(
        functools.partial(exchange_kernel, n, groups, rounds, chunk),
        out_shape=(
            grad, grad,
            jax.ShapeDtypeStruct((rounds * chunk, rows), jnp.bfloat16),
            jax.ShapeDtypeStruct((rounds * chunk, width), images.dtype),
            jax.ShapeDtypeStruct((1, 128), jnp.float32),
        ),
        in_specs=[hbm, smem, smem, hbm, hbm, hbm],
        out_specs=(vmem,) * 5,
        scratch_shapes=[
            pltpu.SMEM((rounds, n), jnp.int32),
            pltpu.VMEM((1, rows), jnp.int32),
            dma((2,)),
            pltpu.VMEM((2, rows, width), images.dtype),
            pltpu.VMEM((chunks // 2, 2, rounds, chunk, width), images.dtype),
            pltpu.VMEM((chunks, rounds, chunk, width), images.dtype),
            pltpu.VMEM((8, 128), jnp.float32),
            pltpu.VMEM((2, 1, 128), jnp.float32),
            pltpu.VMEM((inner_count * groups, 1, 128), jnp.float32),
            pltpu.VMEM((n * groups - 1, 1, 128), jnp.float32),
            dma((chunks,)),
            dma((chunks,)),
            dma((chunks,)),
            dma((2,)),
            dma,
            dma((chunks,)),
            dma((chunks,)),
            dma,
            dma((chunks,)),
            dma,
            dma,
            dma,
            dma,
            regular,
            regular,
            regular,
            regular,
        ]
        + [pltpu.VMEM((n, chunk, width), images.dtype) for _ in range(chunks)],
        compiler_params=pltpu.CompilerParams(
            collective_id=0, has_side_effects=True, vmem_limit_bytes=VMEM_LIMIT
        ),
    )(
        keep(partners), logit_scale, logit_bias,
        keep(labels), keep(images), keep(texts),
    )
    image_grad, text_grad, loss = pl.pallas_call(
        functools.partial(finish_kernel, n * groups * rows),
        out_shape=(grad, grad, jax.ShapeDtypeStruct((1, 1), jnp.float32)),
        in_specs=[smem] + [vmem] * 5,
        out_specs=(hbm, hbm, hbm),
        scratch_shapes=[
            pltpu.VMEM((rows, width), jnp.float32),
            pltpu.SMEM((1, 1), jnp.float32),
            dma,
            dma((FINISH_STEPS,)),
            dma,
        ],
        compiler_params=pltpu.CompilerParams(vmem_limit_bytes=FINISH_LIMIT),
    )(logit_scale, image_sum, text_sum, weight, tail, loss_sum)
    return image_grad, text_grad, loss.reshape(())


def solution(mesh):
    in_specs = (P("grp", "blk", None), P("grp", "blk", None), P("grp", "blk", None), P(), P(), P())
    out_specs = (P("grp", "blk", None), P("grp", "blk", None), P())
    n, groups = mesh.shape["blk"], mesh.shape["grp"]

    def body(images, texts, labels, partners, logit_scale, logit_bias):
        _, rows, width = images.shape
        rounds = partners.shape[0]
        block = 2 * rows * width * images.dtype.itemsize
        needed = block * (n + 3 * rounds + 1) + 2 * rows * width * 4
        fits = needed <= VMEM_BUDGET and n == 2 * LINE_CHIPS and groups > 1
        chunked = rows % (2 * CHUNK_ROWS * GROUP_CHUNKS) == 0 and rows % 128 == 0
        if fits and chunked and width % 128 == 0:
            return line_body(
                n, groups, images, texts, labels, partners, logit_scale, logit_bias
            )
        return spread_body(images, texts, labels, partners, logit_scale, logit_bias)

    return jax.shard_map(body, mesh=mesh, in_specs=in_specs, out_specs=out_specs, check_vma=False)
```

time: 70.5 us -> 67.4 us (0.956)
  Pallas kernels: 68.2 us -> 65.1 us
    pallas_call x1, Pallas kernels: 66.7 us -> 63.7 us  [line_body(): pl.pallas_call(functools.partial(exchange_kernel, n, groups, rounds, chun...]
where the time goes in v3:
time: 67.4 us; the launch traced here: 67.1 us
  Pallas kernels  65.1 us (97%)
  between operations  1.93 us (3%)
    pallas_call x1, Pallas kernels, line_body(): pl.pallas_call(functools.partial(exchange_kernel, n, groups, rounds, chun...  63.7 us
    pallas_call x1, Pallas kernels, line_body(): pl.pallas_call(functools.partial(finish_kernel, n * groups * rows), out_s...  1.45 us

profile of v3, /device:TPU:0, one launch (start us, length us, event | category | flops | bytes accessed | tf_op | source)
XLA Modules:
  0.0 67.1 jit_solution(12990045326985234133)
XLA Ops:
  1.9 63.7 %shard_map.85 = (f32[1,256,1152]{2,1,0:T(8,128)S(1)}, f32[1,256,1152]{2,1,0:T(8,128)S(1)}, bf16[32,256]{1,0:T(8,128)(2,1)S(1)}, bf16[32,1152]{1,0:T(8,128)(2,1)S(1)}, f32[1,128]{1,0:T(1,128)S(1)}) custom-call(s32[2,8]{1,0:T(2,128)} %partners_in.1, f32[]{:T(128)S(6)} %copy.9.scale_ref, f32[]{:T(128)S(6)} %copy.10.bias_ref, s32[1,1,256]{2,1,0:T(1,128)} %labels_in.1, ...), custom_call_target="tpu_custom_call" | custom-call | tf_op jit(solution)/shard_map/pallas_call | solution.py:444
  65.6 1.4 %shard_map.86 = (f32[1,256,1152]{2,1,0:T(8,128)}, f32[1,256,1152]{2,1,0:T(8,128)}, f32[1,1]{1,0:T(1,128)}) custom-call(f32[]{:T(128)S(6)} %copy.9.scale_ref, f32[1,256,1152]{2,1,0:T(8,128)S(1)} %get-tuple-element.11.image_in, f32[1,256,1152]{2,1,0:T(8,128)S(1)} %get-tuple-element.12.text_in, bf16[32,256]{1,0:T(8,128)(2,1)S(1)} %get-tuple-element.13.weight, ...), custom_call_target="tpu_custom_call" | custom-call | tf_op jit(solution)/shard_map/pallas_call | solution.py:491

commit v4 on v3

--- a/solution.py
+++ b/solution.py
@@ -9,7 +9,7 @@
 MESH = pl.DeviceIdType.MESH
 CHUNK_ROWS = 16
 GROUP_CHUNKS = 4
-AHEAD_CHUNKS = 12
+AHEAD_CHUNKS = 8
 LINE_CHIPS = 4
 VMEM_BUDGET = 48 * 1024 * 1024
 VMEM_LIMIT = 32 * 1024 * 1024

time: 67.4 us -> 67.4 us (level)
  no operation moved by 1% of the time
where the time goes in v4:
time: 67.4 us; the launch traced here: 67.1 us
  Pallas kernels  65.1 us (97%)
  between operations  1.93 us (3%)
    pallas_call x1, Pallas kernels, line_body(): pl.pallas_call(functools.partial(exchange_kernel, n, groups, rounds, chun...  63.7 us
    pallas_call x1, Pallas kernels, line_body(): pl.pallas_call(functools.partial(finish_kernel, n * groups * rows), out_s...  1.45 us

profile of v4, /device:TPU:0, one launch (start us, length us, event | category | flops | bytes accessed | tf_op | source)
XLA Modules:
  0.0 67.1 jit_solution(10849702001867258147)
XLA Ops:
  1.9 63.7 %shard_map.85 = (f32[1,256,1152]{2,1,0:T(8,128)S(1)}, f32[1,256,1152]{2,1,0:T(8,128)S(1)}, bf16[32,256]{1,0:T(8,128)(2,1)S(1)}, bf16[32,1152]{1,0:T(8,128)(2,1)S(1)}, f32[1,128]{1,0:T(1,128)S(1)}) custom-call(s32[2,8]{1,0:T(2,128)} %partners_in.1, f32[]{:T(128)S(6)} %copy.9.scale_ref, f32[]{:T(128)S(6)} %copy.10.bias_ref, s32[1,1,256]{2,1,0:T(1,128)} %labels_in.1, ...), custom_call_target="tpu_custom_call" | custom-call | tf_op jit(solution)/shard_map/pallas_call | solution.py:444
  65.6 1.4 %shard_map.86 = (f32[1,256,1152]{2,1,0:T(8,128)}, f32[1,256,1152]{2,1,0:T(8,128)}, f32[1,1]{1,0:T(1,128)}) custom-call(f32[]{:T(128)S(6)} %copy.9.scale_ref, f32[1,256,1152]{2,1,0:T(8,128)S(1)} %get-tuple-element.11.image_in, f32[1,256,1152]{2,1,0:T(8,128)S(1)} %get-tuple-element.12.text_in, bf16[32,256]{1,0:T(8,128)(2,1)S(1)} %get-tuple-element.13.weight, ...), custom_call_target="tpu_custom_call" | custom-call | tf_op jit(solution)/shard_map/pallas_call | solution.py:491
